TPU v7x, 512 devices: a whole 4x4x16 slice. The times are simulated.
512 devices in a mesh: fsdp: 32 (over y, x, core), seq: 16 (over z).
Axes of the slice: x: 4, y: 4, z: 16, core: 2. Of those that a mesh axis runs over, the one named last changes fastest.
Arguments:
- query_rows: bfloat16 [64, 3072, 16, 128], P('fsdp', 'seq'), may hold values from -6 to 6
- key_rows: bfloat16 [64, 3072, 16, 128], P('fsdp', 'seq'), may hold values from -6 to 6
- value_rows: bfloat16 [64, 3072, 16, 128], P('fsdp', 'seq'), may hold values from -6 to 6
- gate_rows: bfloat16 [64, 3072, 16, 128], P('fsdp', 'seq'), may hold values from -6 to 6
- out_weight: bfloat16 [2048, 2048], P('fsdp'), may hold values from -0.125 to 0.125
Outputs:
- block_out: bfloat16 [64, 3072, 2048], P('fsdp', 'seq')
All inputs are finite; a program needn't handle non-finite values.
Results may differ from a plain program's by a relative error of at most 0.006.
Values may be sent and summed in bfloat16 or wider, within the bound.
A program may use at most 64 MiB of HBM per device.

v0:
```python
import jax
import jax.numpy as jnp
from jax import lax
from jax.sharding import PartitionSpec as P


def feature_map(values):
    wide = values.astype(jnp.float32)
    return (wide * wide + 0.1).astype(jnp.bfloat16)


def finish_heads(read, gate_rows, count):
    result = read * count**0.5
    result = result * jax.nn.sigmoid(gate_rows.astype(jnp.float32))
    return result.astype(jnp.bfloat16)


def read_state(features, state, mass):
    top = jnp.einsum(
        "bthd,bhde->bthe", features, state.astype(jnp.bfloat16), preferred_element_type=jnp.float32
    )
    bottom = jnp.einsum("bthd,bhd->bth", features.astype(jnp.float32), mass)
    return top / (bottom + 0.001)[..., None]


def local(query_rows, key_rows, value_rows, gate_rows, out_weight):
    query_feature, key_feature = (feature_map(query_rows), feature_map(key_rows))
    count = query_rows.shape[1] * lax.axis_size("seq")
    part_state = jnp.einsum(
        "bthd,bthe->bhde", key_feature, value_rows, preferred_element_type=jnp.float32
    )
    part_mass = jnp.sum(key_feature.astype(jnp.float32), axis=1)
    state, mass = lax.psum((part_state, part_mass), "seq")
    read = read_state(query_feature, state / count, mass / count)
    mixed = finish_heads(read, gate_rows, count)
    mixed = mixed.reshape(mixed.shape[0], mixed.shape[1], -1)
    return jnp.einsum(
        "btw,wv->btv",
        mixed,
        lax.all_gather(out_weight, "fsdp", axis=0, tiled=True),
        preferred_element_type=jnp.float32,
    ).astype(jnp.bfloat16)


def solution(mesh):
    in_specs = (
        P("fsdp", "seq", None, None),
        P("fsdp", "seq", None, None),
        P("fsdp", "seq", None, None),
        P("fsdp", "seq", None, None),
        P("fsdp", None),
    )
    out_specs = P("fsdp", "seq", None)
    return jax.shard_map(local, mesh=mesh, in_specs=in_specs, out_specs=out_specs, check_vma=False)
```

profile of v0, /device:TPU:2, one launch (start us, length us, event | category | flops | bytes accessed | tf_op | source)
XLA Modules:
  0.0 181.7 jit_solution(9893611185012814220)
XLA Ops:
  7.4 0.0 copy-start
  7.4 0.0 all-reduce.2.cloned.1.call-start
  7.4 2.0 %add_convert_fusion.1 = (bf16[2,192,16,128]{3,2,1,0:T(8,128)(2,1)S(1)}, f32[2,16,128]{2,1,0:T(8,128)S(1)}) fusion(bf16[2,192,16,128]{3,2,1,0:T(8,128)(2,1)} %param.6), kind=kLoop, calls=%fused_computation.8 | loop fusion | flops 4714496 | bytes 3162112 | tf_op jit(solution)/shard_map/convert_element_type | solution.py:9
  9.4 0.0 copy-done
  9.4 2.1 %fusion.10 = f32[2,16,128,128]{3,2,1,0:T(8,128)} fusion(bf16[2,192,16,128]{3,2,1,0:T(8,128)(2,1)S(1)} %copy-done, bf16[2,192,16,128]{3,2,1,0:T(8,128)(2,1)S(1)} %get-tuple-element.5), kind=kOutput, calls=%fused_computation.13 | convolution fusion | flops 201326592 | bytes 5242880 | tf_op jit(solution)/shard_map/bthd,bthe->bhde/dot_general | solution.py:29
  11.6 0.0 all-reduce.2.cloned.1.call-update
  11.6 0.0 all-gather.2.cloned.1.call-start
  11.6 0.5 all-gather.2.cloned.1.call-update
  12.2 62.1 %psum.15 = f32[2,16,128]{2,1,0:T(8,128)S(1)} all-reduce(f32[2,16,128]{2,1,0:T(8,128)S(1)} %get-tuple-element.6), channel_id=1, replica_groups=mesh['fsdp'=32,'seq'=16] {'seq'}, use_global_device_ids=true, to_apply=%region_2.0 | all-reduce | flops 4096 | bytes 32768 | tf_op jit(solution)/shard_map/psum | solution.py:33
  74.2 1.9 %add_convert_fusion = bf16[2,192,16,128]{3,2,1,0:T(8,128)(2,1)S(1)} fusion(bf16[2,192,16,128]{3,2,1,0:T(8,128)(2,1)} %param.5), kind=kLoop, calls=%fused_computation.7 | loop fusion | flops 3145728 | bytes 3145728 | tf_op jit(solution)/shard_map/convert_element_type | solution.py:9
  76.1 0.9 fusion.14
  77.0 83.5 %all-reduce.2.cloned.1.call-done = f32[2,16,128,128]{3,2,1,0:T(8,128)} async-done(((f32[2,16,128,128]{3,2,1,0:T(8,128)}), f32[2,16,128,128]{3,2,1,0:T(8,128)}) %all-reduce.2.cloned.1.call-update) | async-done | bytes 2097168 | tf_op jit(solution)/shard_map/psum | solution.py:33
  160.6 5.3 %fusion.13 = bf16[2,16,24,8,128]{4,3,2,1,0:T(8,128)(2,1)} fusion(bf16[2,192,16,128]{3,2,1,0:T(8,128)(2,1)} %param.8, f32[2,192,16]{1,2,0:T(8,128)S(1)} %fusion.18, bf16[2,192,16,128]{3,2,1,0:T(8,128)(2,1)S(1)} %add_convert_fusion, f32[2,16,128,128]{3,2,1,0:T(8,128)} %all-reduce.2.cloned.1.call-done), kind=kOutput, calls=%fused_computation.16 | convolution fusion | flops 208666624 | bytes 6840320 | tf_op jit(solution)/shard_map/bthd,bhde->bthe/dot_general | solution.py:19
  165.9 0.0 all-gather.2.cloned.1.call-done
  165.9 8.4 %fusion.5 = bf16[2,192,2048]{2,1,0:T(8,128)(2,1)} fusion(bf16[2048,2048]{1,0:T(8,128)(2,1)} %all-gather.2.cloned.1.call-done, bf16[2,16,24,8,128]{4,3,2,1,0:T(8,128)(2,1)} %fusion.13), kind=kOutput, calls=%fused_computation.9 | convolution fusion | flops 3222011904 | bytes 11534336 | tf_op jit(solution)/shard_map/btw,wv->btv/dot_general | solution.py:37
  (2 shorter events, 0.0 us)
Async XLA Ops:
  7.4 2.0 %copy-start = (bf16[2,192,16,128]{3,2,1,0:T(8,128)(2,1)S(1)}, bf16[2,192,16,128]{3,2,1,0:T(8,128)(2,1)}, u32[]{:S(2)}) copy-start(bf16[2,192,16,128]{3,2,1,0:T(8,128)(2,1)} %param.7) | copy-start | bytes 4718596
  7.4 153.2 %all-reduce.2.cloned.1.call-start = ((), (), s32[]{:S(2)}) async-start(), calls=%async_computation | async-start | bytes 4194304 | tf_op jit(solution)/shard_map/psum | solution.py:33
  11.6 154.3 %all-gather.2.cloned.1.call-start = ((), (), s32[]{:S(2)}) async-start(), calls=%async_computation.1 | async-start | bytes 8650752 | tf_op jit(solution)/shard_map/all_gather | solution.py:40
Sparse Core Ops, SparseCore 0:
  11.7 148.8 all-reduce.1
Sparse Core Ops, SparseCore 1:
  15.2 72.4 all-gather.1
where the time goes:
time: 182 us
  waiting for transfers between devices  84.1 us (46%)
  blocking collectives  62.1 us (34%)
  matrix products  16.7 us (9%)
  between operations  14.9 us (8%)
  other arithmetic  3.94 us (2%)
    psum x1, waiting for transfers between devices, local(): state, mass = lax.psum((part_state, part_mass), 'seq')  83.5 us
    psum x1, blocking collectives, local(): state, mass = lax.psum((part_state, part_mass), 'seq')  62.1 us
    dot_general x1, matrix products, local(): jnp.einsum('btw,wv->btv', mixed, lax.all_gather(out_weight, 'fsdp', axis=...  8.42 us
    dot_general x1, matrix products, read_state(): jnp.einsum('bthd,bhde->bthe', features, state.astype(jnp.bfloat16), prefe...  5.28 us
    convert_element_type x2, other arithmetic, feature_map(): return (wide * wide + 0.1).astype(jnp.bfloat16)  3.93 us
  transfers between devices with their start and end apart: 2, of which 1 were waited for; matrix products, arithmetic and copies ran while one was open for 4% of the time, Pallas kernels for 0%

commit v1 on v0

v1 whole, which is shorter than its diff:
```python
import functools

import jax
import jax.numpy as jnp
from jax import lax
from jax.experimental import pallas as pl
from jax.experimental.pallas import tpu as pltpu
from jax.sharding import PartitionSpec as P

MESH = pl.DeviceIdType.MESH
F32, BF16 = jnp.float32, jnp.bfloat16
BLOCK = 32
UP, DOWN = 0, 1


def feature(raw):
    wide = raw.astype(F32)
    return wide * wide + 0.1


def layer_kernel(
    ny, nx, nz, count,
    q_hbm, k_hbm, v_hbm, g_hbm, w_hbm, out_ref,
    q_raw, k_raw, v_raw, g_raw, q_feat, k_feat, v_head, gates,
    part, other, sums, states, weight, mixed, total,
    load_sem, part_send, part_recv, rs_send, rs_recv, ag_send, ag_recv,
    hand_send, hand_recv, line_send, line_recv, push_send, push_recv, own_send, own_recv,
):
    seqs, tokens, heads, size = k_raw.shape
    width = weight.shape[2]
    half = weight.shape[1] // 2
    state_rows = 2 * seqs * size
    z, f = lax.axis_index("seq"), lax.axis_index("fsdp")
    core = lax.rem(f, 2)
    chip = f // 2
    x, y = lax.rem(chip, nx), chip // nx
    above, below = lax.rem(z + 1, nz), lax.rem(z + nz - 1, nz)
    partner = {"fsdp": chip * 2 + 1 - core}
    barrier = pltpu.get_barrier_semaphore()

    def head_at(offset):
        return lax.rem(z + offset + 2 * nz, nz)

    loads = [
        pltpu.make_async_copy(src, dst, load_sem.at[at])
        for at, (src, dst) in enumerate(((k_hbm, k_raw), (v_hbm, v_raw), (q_hbm, q_raw), (g_hbm, g_raw)))
    ]
    own_rows = weight.at[chip, pl.ds(pl.multiple_of(core * half, half), half)]
    loads.append(pltpu.make_async_copy(w_hbm, own_rows, load_sem.at[4]))

    def by_head(values):
        return jnp.swapaxes(values, 0, 1)

    def relayout(s, t):
        rows = pl.ds(pl.multiple_of(t, BLOCK), BLOCK)
        k_feat[:, s, rows, :] = by_head(feature(k_raw[s, rows])).astype(BF16)
        v_head[:, s, rows, :] = by_head(v_raw[s, rows].astype(F32)).astype(BF16)

    def relayout_all():
        for s in range(seqs):
            @pl.loop(0, tokens // BLOCK)
            def _(i):
                relayout(s, i * BLOCK)

    def relayout_late(unit):
        per_seq = tokens // BLOCK
        s = unit // per_seq
        rows = pl.ds(pl.multiple_of(lax.rem(unit, per_seq) * BLOCK, BLOCK), BLOCK)
        q_feat[:, s, rows, :] = by_head(feature(q_raw[s, rows])).astype(BF16)
        gate = g_raw[s, rows].astype(F32)
        gates[:, s, rows, :] = by_head(count**0.5 / (1.0 + jnp.exp(-gate)))

    late_units = seqs * tokens // BLOCK

    def partial(head, first_row):
        ones = jnp.ones((8, tokens), BF16)
        place = lax.broadcasted_iota(jnp.int32, (8, size), 0)
        mass = jnp.zeros((8, size), F32)
        for s in range(seqs):
            keys = k_feat[head, s]
            part[head, s * size:(s + 1) * size, :] = lax.dot_general(
                keys, v_head[head, s], (((0,), (0,)), ((), ())), preferred_element_type=F32
            )
            row = jnp.dot(ones, keys, preferred_element_type=F32)
            mass = jnp.where(place == first_row + s, row, mass)
        part[head, seqs * size:, :] = mass

    def read_head(head, first_row):
        tail = states[head, state_rows:, :].astype(F32)
        for s in range(seqs):
            row = first_row + s
            feats = q_feat[head, s]
            top = jnp.dot(
                feats, states[head, row * size:(row + 1) * size, :], preferred_element_type=F32
            )
            mass = tail[row:row + 1] + tail[8 + row:9 + row]
            bottom = jnp.sum(feats.astype(F32) * mass, axis=1, keepdims=True)
            read = top * (1.0 / (bottom + 0.001))
            mixed[head, s * tokens:(s + 1) * tokens, :] = (read * gates[head, s]).astype(BF16)

    def project(a, b, first=False, last=False):
        rows = jnp.concatenate([mixed[a], mixed[b]], axis=1)
        step = 512

        @pl.loop(0, width // step)
        def _(i):
            cols = pl.ds(pl.multiple_of(i * step, step), step)
            piece = jnp.dot(
                rows, jnp.concatenate([weight[a, :, cols], weight[b, :, cols]], axis=0),
                preferred_element_type=F32,
            )
            if not first:
                piece = total[:, cols] + piece
            if last:
                for s in range(seqs):
                    out_ref[s, :, cols] = piece[s * tokens:(s + 1) * tokens].astype(BF16)
            else:
                total[:, cols] = piece

    def part_copy(head):
        return pltpu.make_async_remote_copy(
            part.at[head], other.at[head], part_send.at[head], part_recv.at[head],
            device_id=partner, device_id_type=MESH,
        )

    def hand_copy(head):
        rows = pl.ds(seqs * size, state_rows + 16 - seqs * size)
        return pltpu.make_async_remote_copy(
            states.at[head, rows], states.at[head, rows], hand_send.at[head], hand_recv.at[head],
            device_id=partner, device_id_type=MESH,
        )

    def push_copy(piece, which):
        rows = pl.ds(which * half, half)
        return pltpu.make_async_remote_copy(
            weight.at[piece, rows], weight.at[piece, rows],
            push_send.at[piece, which], push_recv.at[piece, which],
            device_id=partner, device_id_type=MESH,
        )

    def own_copy():
        return pltpu.make_async_remote_copy(
            w_hbm, weight.at[chip, pl.ds(half, half)], own_send, own_recv,
            device_id=partner, device_id_type=MESH,
        )

    @pl.when(core == 1)
    def _ring():
        for load in loads:
            load.start()
        for device in ({"seq": above}, {"seq": below}, partner):
            pl.semaphore_signal(barrier, inc=1, device_id=device, device_id_type=MESH)
        loads[0].wait()
        loads[1].wait()
        relayout_all()
        partial(head_at(nz // 2), 0)
        pl.semaphore_wait(barrier, 3)
        own_copy().start()

        pieces = 2 * seqs
        spans = [(i * size, size if i < pieces - 1 else size + 16) for i in range(pieces)]
        early = jnp.where(lax.rem(z, 4) < 2, DOWN, UP)

        def target(d):
            return {"seq": jnp.where(d == UP, above, below)}

        def rs_copy(k, d, i):
            rows = pl.ds(*spans[i])
            return pltpu.make_async_remote_copy(
                sums.at[d, k, rows], sums.at[d, k + 1, rows], rs_send.at[k, d, i], rs_recv.at[k, d, i],
                device_id=target(d), device_id_type=MESH,
            )

        def ag_copy(k, d, i):
            rows = pl.ds(*spans[i])
            head = head_at(jnp.where(d == UP, -k, k))
            return pltpu.make_async_remote_copy(
                states.at[head, rows], states.at[head, rows], ag_send.at[k, d, i], ag_recv.at[k, d, i],
                device_id=target(d), device_id_type=MESH,
            )

        def ag_arrived(k, d, i):
            rows = pl.ds(*spans[i])
            head = head_at(jnp.where(d == UP, -k - 1, k + 1))
            pltpu.make_async_remote_copy(
                states.at[head, rows], states.at[head, rows], ag_send.at[k, d, i], ag_recv.at[k, d, i],
                device_id=target(d), device_id_type=MESH,
            ).wait_recv()

        def own_sum(head, i):
            if i < seqs:
                return part[head, i * size:(i + 1) * size, :]
            return other[head, (i - seqs) * size:(i - seqs + 1) * size, :]

        def own_mass(head):
            return part[head, seqs * size:, :] + other[head, seqs * size:, :]

        def split(mass):
            high = mass.astype(BF16)
            return jnp.concatenate([high.astype(F32), mass - high.astype(F32)], axis=0).astype(BF16)

        def add_and_send(k, d, i, received):
            head = head_at(jnp.where(d == UP, nz // 2 - k, nz // 2 + k))
            start = i * size
            value = own_sum(head, i)
            if received:
                rs_copy(k - 1, d, i).wait_recv()
                value = value + sums[d, k, start:start + size, :].astype(F32)
            sums[d, k, start:start + size, :] = value.astype(BF16)
            if i == pieces - 1:
                mass = own_mass(head)
                if received:
                    old = sums[d, k, state_rows:, :].astype(F32)
                    mass = mass + old[:8] + old[8:]
                sums[d, k, state_rows:, :] = split(mass)
            rs_copy(k, d, i).start()

        def first_way(i):
            return DOWN if i < seqs else UP

        for i in range(pieces):
            if i == seqs:
                part_copy(head_at(nz // 2)).wait_recv()
            add_and_send(0, first_way(i), i, False)
        partial(head_at(nz // 2 + 1), 0)
        partial(head_at(nz // 2 - 1), 0)
        for i in range(pieces):
            if i == seqs:
                part_copy(head_at(nz // 2 + 1)).wait_recv()
                part_copy(head_at(nz // 2 - 1)).wait_recv()
            add_and_send(1, 1 - first_way(i), i, False)
            add_and_send(1, first_way(i), i, True)
        partial(head_at(nz // 2 + 2), 0)
        partial(head_at(nz // 2 - 2), 0)
        loads[2].wait()
        loads[3].wait()

        per_step = -(-late_units // (nz // 2 - 2))

        @pl.loop(2, nz // 2)
        def _(k):
            for i in range(pieces):
                if i == seqs:
                    part_copy(head_at(nz // 2 + k)).wait_recv()
                    part_copy(head_at(nz // 2 - k)).wait_recv()
                add_and_send(k, early, i, True)
                add_and_send(k, 1 - early, i, True)

            @pl.when(k < nz // 2 - 1)
            def _():
                partial(head_at(nz // 2 + k + 1), 0)
                partial(head_at(nz // 2 - k - 1), 0)

            @pl.when(k == nz // 2 - 1)
            def _():
                partial(head_at(0), 0)

            for j in range(per_step):
                relayout_late((k - 2) * per_step + j)

        order = list(range(seqs, pieces)) + list(range(seqs))
        part_copy(z).wait_recv()
        for i in order:
            start = i * size
            value = own_sum(z, i)
            for d in (DOWN, UP):
                rs_copy(nz // 2 - 1, d, i).wait_recv()
                value = value + sums[d, nz // 2, start:start + size, :].astype(F32)
            states[z, start:start + size, :] = (value * (1.0 / count)).astype(BF16)
            if i == pieces - 1:
                mass = own_mass(z)
                for d in (DOWN, UP):
                    old = sums[d, nz // 2, state_rows:, :].astype(F32)
                    mass = mass + old[:8] + old[8:]
                states[z, state_rows:, :] = split(mass * (1.0 / count))
            ag_copy(0, UP, i).start()
            ag_copy(0, DOWN, i).start()
            if i == pieces - 1:
                hand_copy(z).start()

        def pass_on(k, both):
            for i in order:
                if both:
                    for d in (early, 1 - early):
                        ag_arrived(k - 1, d, i)
                        ag_copy(k, d, i).start()
                else:
                    for d in (UP, DOWN):
                        ag_arrived(k - 1, d, i)
                    ag_copy(k, 1 - first_way(i), i).start()
                if i == pieces - 1:
                    hand_copy(head_at(-k)).start()
                    hand_copy(head_at(k)).start()

        def weights_here():
            for offset in range(nx * ny):
                piece = lax.rem(chip + offset, nx * ny)
                push_copy(piece, 0).wait_recv()
                if offset > 0:
                    push_copy(piece, 1).wait_recv()

        def read_pair(k):
            read_head(head_at(-k), 0)
            read_head(head_at(k), 0)

        pass_on(1, True)
        read_head(z, 0)
        read_pair(1)
        pass_on(2, True)
        read_pair(2)
        loads[4].wait()
        weights_here()
        project(head_at(-1), head_at(1), first=True)

        @pl.loop(3, nz // 2 - 1)
        def _(k):
            pass_on(k, True)
            read_pair(k)
            project(head_at(1 - k), head_at(k - 1))

        pass_on(nz // 2 - 1, False)
        read_pair(nz // 2 - 1)
        project(head_at(2 - nz // 2), head_at(nz // 2 - 2))
        for i in order:
            ag_arrived(nz // 2 - 1, 1 - first_way(i), i)
            if i == pieces - 1:
                hand_copy(head_at(nz // 2)).start()
        project(head_at(1 - nz // 2), head_at(nz // 2 - 1))
        read_head(head_at(nz // 2), 0)
        project(z, head_at(nz // 2), last=True)

        own_copy().wait_send()
        for i in range(pieces):
            rs_copy(0, first_way(i), i).wait_send()
            ag_copy(nz // 2 - 1, 1 - first_way(i), i).wait_send()

        @pl.loop(0, nz // 2 - 1)
        def _(k):
            for i in range(pieces):
                for d in (UP, DOWN):
                    rs_copy(k + 1, d, i).wait_send()
                    ag_copy(k, d, i).wait_send()

        @pl.loop(0, nz)
        def _(j):
            hand_copy(j).wait_send()

    @pl.when(core == 0)
    def _weights():
        for load in loads:
            load.start()
        east, west = y * nx + lax.rem(x + 1, nx), y * nx + lax.rem(x + nx - 1, nx)
        north, south = lax.rem(y + 1, ny) * nx + x, lax.rem(y + ny - 1, ny) * nx + x
        ways = ((east, west), (north, south))
        for device in (east, west, north, south):
            pl.semaphore_signal(barrier, inc=1, device_id={"fsdp": device * 2}, device_id_type=MESH)
        pl.semaphore_signal(barrier, inc=1, device_id=partner, device_id_type=MESH)

        items = (((0, 0), (1, 0), (1, -1), (1, 1), (1, 2)), ((1, 0), (0, 0), (0, -1), (0, 1), (0, 2)))

        def piece_at(axis, item, along):
            across = items[axis][item][1]
            dx, dy = (along, across) if axis == 0 else (across, along)
            return lax.rem(y + dy + ny, ny) * nx + lax.rem(x + dx + nx, nx)

        def line_copy(axis, item, way, stage, arriving):
            sign = 1 if way == 0 else -1
            if stage == 0:
                along, start, rows = 0, 0, half
            else:
                along, start, rows = -sign, way * (half // 2), half // 2
            if arriving:
                along = along - sign
                along = 2 if along == -2 else along
            spot = weight.at[piece_at(axis, item, along), pl.ds(items[axis][item][0] * half + start, rows)]
            return pltpu.make_async_remote_copy(
                spot, spot, line_send.at[axis, item, way, stage], line_recv.at[axis, item, way, stage],
                device_id={"fsdp": ways[axis][way] * 2}, device_id_type=MESH,
            )

        def send(axis, item):
            for way in (0, 1):
                line_copy(axis, item, way, 0, False).start()

        def got(axis, item, stage):
            for way in (0, 1):
                line_copy(axis, item, way, stage, True).wait_recv()

        def forward(axis, item):
            for way in (0, 1):
                line_copy(axis, item, way, 0, True).wait_recv()
                line_copy(axis, item, way, 1, False).start()

        def at(dx, dy):
            return lax.rem(y + dy + ny, ny) * nx + lax.rem(x + dx + nx, nx)

        def push(dx, dy, which):
            push_copy(at(dx, dy), which).start()

        loads[0].wait()
        loads[1].wait()
        relayout_all()
        pl.semaphore_wait(barrier, 5)
        loads[4].wait()
        send(0, 0)
        send(1, 1)

        def part_out(offset):
            partial(head_at(offset), seqs)
            part_copy(head_at(offset)).start()

        part_out(nz // 2)

        @pl.loop(1, nz // 2)
        def _(k):
            part_out(nz // 2 + k)
            part_out(nz // 2 - k)

            @pl.when(k == 2)
            def _():
                own_copy().wait_recv()
                send(1, 0)
                send(0, 1)

        part_out(0)
        push(0, 0, 0)
        loads[2].wait()
        loads[3].wait()

        @pl.loop(0, late_units // 2)
        def _(i):
            relayout_late(i)

        forward(0, 0)
        send(1, 2)
        send(1, 3)
        push(-1, 0, 0)
        push(1, 0, 0)
        forward(1, 0)
        send(0, 2)
        send(0, 3)
        push(0, -1, 1)
        push(0, 1, 1)

        @pl.loop(late_units // 2, late_units)
        def _(i):
            relayout_late(i)

        forward(0, 1)
        forward(1, 1)
        push(-1, 0, 1)
        push(1, 0, 1)
        push(0, -1, 0)
        push(0, 1, 0)
        got(0, 0, 1)
        send(1, 4)
        push(2, 0, 0)
        got(1, 0, 1)
        send(0, 4)
        push(0, 2, 1)
        for item, off in ((2, -1), (3, 1)):
            forward(1, item)
            push(off, -1, 0)
            push(off, 1, 0)
            forward(0, item)
            push(-1, off, 1)
            push(1, off, 1)
        got(0, 1, 1)
        push(2, 0, 1)
        got(1, 1, 1)
        push(0, 2, 0)
        forward(1, 4)
        push(2, -1, 0)
        push(2, 1, 0)
        forward(0, 4)
        push(-1, 2, 1)
        push(1, 2, 1)
        for item, off in ((2, -1), (3, 1), (4, 2)):
            got(1, item, 1)
            push(off, 2, 0)
            got(0, item, 1)
            push(2, off, 1)

        hand_copy(z).wait_recv()
        read_head(z, seqs)

        def read_pair(k):
            for head in (head_at(-k), head_at(k)):
                hand_copy(head).wait_recv()
                read_head(head, seqs)

        read_pair(1)
        project(head_at(-1), head_at(1), first=True)

        @pl.loop(2, nz // 2)
        def _(k):
            read_pair(k)
            project(head_at(-k), head_at(k))

        hand_copy(head_at(nz // 2)).wait_recv()
        read_head(head_at(nz // 2), seqs)
        project(z, head_at(nz // 2), last=True)

        for axis in (0, 1):
            for item in range(5):
                for way in (0, 1):
                    for stage in (0, 1):
                        line_copy(axis, item, way, stage, False).wait_send()

        @pl.loop(0, nz)
        def _(j):
            part_copy(j).wait_send()

        for offset in range(nx * ny):
            piece = lax.rem(chip + offset, nx * ny)
            push_copy(piece, 0).wait_send()
            if offset > 0:
                push_copy(piece, 1).wait_send()


def local(ny, nx, nz, query_rows, key_rows, value_rows, gate_rows, out_weight):
    seqs, tokens, heads, size = query_rows.shape
    rows, width = out_weight.shape
    chips = nx * ny
    raw = pltpu.VMEM((seqs, tokens, heads, size), BF16)
    split = pltpu.VMEM((heads, seqs, tokens, size), BF16)
    part = pltpu.VMEM((heads, seqs * size + 8, size), F32)
    chunk = 2 * seqs * size + 16
    dma = pltpu.SemaphoreType.DMA
    return pl.pallas_call(
        functools.partial(layer_kernel, ny, nx, nz, float(tokens * nz)),
        name="layer",
        out_shape=jax.ShapeDtypeStruct((seqs, tokens, width), BF16),
        in_specs=[pl.BlockSpec(memory_space=pl.ANY)] * 5,
        out_specs=pl.BlockSpec(memory_space=pltpu.VMEM),
        scratch_shapes=[
            raw, raw, raw, raw,
            split, split, split,
            pltpu.VMEM((heads, seqs, tokens, size), F32),
            part, part,
            pltpu.VMEM((2, nz // 2 + 1, chunk, size), BF16),
            pltpu.VMEM((heads, chunk, size), BF16),
            pltpu.VMEM((chips, 2 * rows, width), BF16),
            pltpu.VMEM((heads, seqs * tokens, size), BF16),
            pltpu.VMEM((seqs * tokens, width), F32),
            dma((5,)),
            dma((heads,)), dma((heads,)),
            dma((nz // 2, 2, 2 * seqs)), dma((nz // 2, 2, 2 * seqs)),
            dma((nz // 2, 2, 2 * seqs)), dma((nz // 2, 2, 2 * seqs)),
            dma((heads,)), dma((heads,)),
            dma((2, 5, 2, 2)), dma((2, 5, 2, 2)),
            dma((chips, 2)), dma((chips, 2)),
            dma, dma,
        ],
        compiler_params=pltpu.CompilerParams(
            collective_id=0, has_side_effects=True, vmem_limit_bytes=60 * 2**20
        ),
    )(query_rows, key_rows, value_rows, gate_rows, out_weight)


def solution(mesh):
    in_specs = (
        P("fsdp", "seq", None, None),
        P("fsdp", "seq", None, None),
        P("fsdp", "seq", None, None),
        P("fsdp", "seq", None, None),
        P("fsdp", None),
    )
    out_specs = P("fsdp", "seq", None)
    body = functools.partial(local, 4, 4, mesh.shape["seq"])
    return jax.shard_map(body, mesh=mesh, in_specs=in_specs, out_specs=out_specs, check_vma=False)
```

time: 182 us -> 68.7 us (0.38)
  the two profiles are of different devices: /device:TPU:2 before, /device:TPU:1 now
where the time goes in v1:
time: 68.7 us; the launch traced here: 68.5 us
  Pallas kernels  65.8 us (96%)
  local copies, waits for them, and re-layouts  2.73 us (4%)
    pallas_call x1, Pallas kernels, local(): pl.pallas_call(functools.partial(layer_kernel, ny, nx, nz, float(tokens *...  65.8 us
    unnamed x1, local copies, waits for them, and re-layouts  2.73 us

profile of v1, /device:TPU:1, one launch (start us, length us, event | category | flops | bytes accessed | tf_op | source)
XLA Modules:
  0.0 68.5 jit_solution(12567212146729560500)
XLA Ops:
  0.0 65.8 %layer.1 = bf16[2,192,2048]{2,1,0:T(8,128)(2,1)} custom-call(bf16[2,192,16,128]{3,2,1,0:T(8,128)(2,1)} %q_hbm.1, bf16[2,192,16,128]{3,2,1,0:T(8,128)(2,1)} %k_hbm.1, bf16[2,192,16,128]{3,2,1,0:T(8,128)(2,1)} %v_hbm.1, bf16[2,192,16,128]{3,2,1,0:T(8,128)(2,1)} %g_hbm.1, bf16[64,2048]{1,0:T(8,128)(2,1)} %w_hbm.1), custom_call_target="tpu_custom_call" | custom-call | tf_op jit(solution)/shard_map/layer/pallas_call | solution.py:530
  65.8 2.7 %copy.7 = bf16[2,192,2048]{2,1,0:T(8,128)(2,1)} copy(bf16[2,192,2048]{2,1,0:T(8,128)(2,1)} %layer.1) | data formatting | bytes 3145728

commit v2 on v1

--- a/solution.py
+++ b/solution.py
@@ -41,26 +41,58 @@
     def head_at(offset):
         return lax.rem(z + offset + 2 * nz, nz)
 
-    loads = [
-        pltpu.make_async_copy(src, dst, load_sem.at[at])
-        for at, (src, dst) in enumerate(((k_hbm, k_raw), (v_hbm, v_raw), (q_hbm, q_raw), (g_hbm, g_raw)))
+    key_loads, value_loads = (
+        [pltpu.make_async_copy(src.at[s], dst.at[s], load_sem.at[at, s]) for s in range(seqs)]
+        for at, (src, dst) in enumerate(((k_hbm, k_raw), (v_hbm, v_raw)))
+    )
+    late_loads = [
+        pltpu.make_async_copy(src, dst, load_sem.at[2, at])
+        for at, (src, dst) in enumerate(((q_hbm, q_raw), (g_hbm, g_raw)))
     ]
     own_rows = weight.at[chip, pl.ds(pl.multiple_of(core * half, half), half)]
-    loads.append(pltpu.make_async_copy(w_hbm, own_rows, load_sem.at[4]))
+    own_load = pltpu.make_async_copy(w_hbm, own_rows, load_sem.at[3, 0])
+
+    def start_loads():
+        for s in range(seqs):
+            key_loads[s].start()
+            value_loads[s].start()
+        own_load.start()
+        for load in late_loads:
+            load.start()
 
     def by_head(values):
         return jnp.swapaxes(values, 0, 1)
 
-    def relayout(s, t):
-        rows = pl.ds(pl.multiple_of(t, BLOCK), BLOCK)
-        k_feat[:, s, rows, :] = by_head(feature(k_raw[s, rows])).astype(BF16)
-        v_head[:, s, rows, :] = by_head(v_raw[s, rows].astype(F32)).astype(BF16)
-
-    def relayout_all():
+    group = heads // 2
+
+    def relayout(which, wait):
+        span = slice(which * group, (which + 1) * group)
         for s in range(seqs):
-            @pl.loop(0, tokens // BLOCK)
-            def _(i):
-                relayout(s, i * BLOCK)
+            for load, src, dst, fn in (
+                (key_loads[s], k_raw, k_feat, feature),
+                (value_loads[s], v_raw, v_head, lambda raw: raw.astype(F32)),
+            ):
+                if wait:
+                    load.wait()
+
+                @pl.loop(0, tokens // BLOCK)
+                def _(i):
+                    rows = pl.ds(pl.multiple_of(i * BLOCK, BLOCK), BLOCK)
+                    dst[span, s, rows, :] = by_head(fn(src[s, rows, span])).astype(BF16)
+
+    starts_late = z >= nz // 2
+
+    def relayout_first():
+        relayout(0, True)
+
+        @pl.when(jnp.logical_not(starts_late))
+        def _():
+            relayout(1, False)
+
+    def relayout_rest():
+        @pl.when(starts_late)
+        def _():
+            relayout(1, False)
 
     def relayout_late(unit):
         per_seq = tokens // BLOCK
@@ -85,37 +117,41 @@
             mass = jnp.where(place == first_row + s, row, mass)
         part[head, seqs * size:, :] = mass
 
+    def read_part(head, first_row, s):
+        tail = states[head, state_rows:, :].astype(F32)
+        row = first_row + s
+        feats = q_feat[head, s]
+        top = jnp.dot(feats, states[head, row * size:(row + 1) * size, :], preferred_element_type=F32)
+        mass = tail[row:row + 1] + tail[8 + row:9 + row]
+        bottom = jnp.sum(feats.astype(F32) * mass, axis=1, keepdims=True)
+        read = top * (1.0 / (bottom + 0.001))
+        mixed[head, s * tokens:(s + 1) * tokens, :] = (read * gates[head, s]).astype(BF16)
+
     def read_head(head, first_row):
-        tail = states[head, state_rows:, :].astype(F32)
         for s in range(seqs):
-            row = first_row + s
-            feats = q_feat[head, s]
-            top = jnp.dot(
-                feats, states[head, row * size:(row + 1) * size, :], preferred_element_type=F32
-            )
-            mass = tail[row:row + 1] + tail[8 + row:9 + row]
-            bottom = jnp.sum(feats.astype(F32) * mass, axis=1, keepdims=True)
-            read = top * (1.0 / (bottom + 0.001))
-            mixed[head, s * tokens:(s + 1) * tokens, :] = (read * gates[head, s]).astype(BF16)
+            read_part(head, first_row, s)
+
+    step = width // 4
+
+    def project_part(a, b, i, first=False, last=False):
+        rows = jnp.concatenate([mixed[a], mixed[b]], axis=1)
+        cols = pl.ds(pl.multiple_of(i * step, step), step)
+        piece = jnp.dot(
+            rows, jnp.concatenate([weight[a, :, cols], weight[b, :, cols]], axis=0),
+            preferred_element_type=F32,
+        )
+        if not first:
+            piece = total[:, cols] + piece
+        if last:
+            for s in range(seqs):
+                out_ref[s, :, cols] = piece[s * tokens:(s + 1) * tokens].astype(BF16)
+        else:
+            total[:, cols] = piece
 
     def project(a, b, first=False, last=False):
-        rows = jnp.concatenate([mixed[a], mixed[b]], axis=1)
-        step = 512
-
         @pl.loop(0, width // step)
         def _(i):
-            cols = pl.ds(pl.multiple_of(i * step, step), step)
-            piece = jnp.dot(
-                rows, jnp.concatenate([weight[a, :, cols], weight[b, :, cols]], axis=0),
-                preferred_element_type=F32,
-            )
-            if not first:
-                piece = total[:, cols] + piece
-            if last:
-                for s in range(seqs):
-                    out_ref[s, :, cols] = piece[s * tokens:(s + 1) * tokens].astype(BF16)
-            else:
-                total[:, cols] = piece
+            project_part(a, b, i, first, last)
 
     def part_copy(head):
         return pltpu.make_async_remote_copy(
@@ -146,13 +182,10 @@
 
     @pl.when(core == 1)
     def _ring():
-        for load in loads:
-            load.start()
+        start_loads()
         for device in ({"seq": above}, {"seq": below}, partner):
             pl.semaphore_signal(barrier, inc=1, device_id=device, device_id_type=MESH)
-        loads[0].wait()
-        loads[1].wait()
-        relayout_all()
+        relayout_first()
         partial(head_at(nz // 2), 0)
         pl.semaphore_wait(barrier, 3)
         own_copy().start()
@@ -222,6 +255,7 @@
             if i == seqs:
                 part_copy(head_at(nz // 2)).wait_recv()
             add_and_send(0, first_way(i), i, False)
+        relayout_rest()
         partial(head_at(nz // 2 + 1), 0)
         partial(head_at(nz // 2 - 1), 0)
         for i in range(pieces):
@@ -232,8 +266,8 @@
             add_and_send(1, first_way(i), i, True)
         partial(head_at(nz // 2 + 2), 0)
         partial(head_at(nz // 2 - 2), 0)
-        loads[2].wait()
-        loads[3].wait()
+        for load in late_loads:
+            load.wait()
 
         per_step = -(-late_units // (nz // 2 - 2))
 
@@ -257,6 +291,8 @@
 
             for j in range(per_step):
                 relayout_late((k - 2) * per_step + j)
+            rows = seqs * tokens // (nz // 2 - 2)
+            total[pl.ds(pl.multiple_of((k - 2) * rows, 8), rows), :] = jnp.zeros((rows, width), F32)
 
         order = list(range(seqs, pieces)) + list(range(seqs))
         part_copy(z).wait_recv()
@@ -278,8 +314,8 @@
             if i == pieces - 1:
                 hand_copy(z).start()
 
-        def pass_on(k, both):
-            for i in order:
+        def pass_on(k, both, work):
+            for slot, i in enumerate(order):
                 if both:
                     for d in (early, 1 - early):
                         ag_arrived(k - 1, d, i)
@@ -291,55 +327,78 @@
                 if i == pieces - 1:
                     hand_copy(head_at(-k)).start()
                     hand_copy(head_at(k)).start()
+                work(k, slot)
 
         def weights_here():
+            own_load.wait()
             for offset in range(nx * ny):
                 piece = lax.rem(chip + offset, nx * ny)
                 push_copy(piece, 0).wait_recv()
                 if offset > 0:
                     push_copy(piece, 1).wait_recv()
 
-        def read_pair(k):
-            read_head(head_at(-k), 0)
-            read_head(head_at(k), 0)
-
-        pass_on(1, True)
-        read_head(z, 0)
-        read_pair(1)
-        pass_on(2, True)
-        read_pair(2)
-        loads[4].wait()
+        def read_slice(k, slot):
+            read_part(head_at(-k) if slot < seqs else head_at(k), 0, slot % seqs)
+
+        def project_slice(k, slot):
+            project_part(head_at(-k), head_at(k), slot)
+
+        def drain(k, slot):
+            i = slot
+            for d in (UP, DOWN):
+                rs_copy(k, d, i).wait_send()
+
+        def first_work(k, slot):
+            drain(k, slot)
+            if slot < seqs:
+                read_part(z, 0, slot)
+
+        def second_work(k, slot):
+            drain(k, slot)
+            read_slice(k - 1, slot)
+
+        def later_work(k, slot):
+            drain(k, slot)
+            read_slice(k - 1, slot)
+            project_slice(k - 2, slot)
+
+        end = nz // 2
+        pass_on(1, True, first_work)
+        pass_on(2, True, second_work)
         weights_here()
-        project(head_at(-1), head_at(1), first=True)
-
-        @pl.loop(3, nz // 2 - 1)
+
+        @pl.loop(3, end - 1)
         def _(k):
-            pass_on(k, True)
-            read_pair(k)
-            project(head_at(1 - k), head_at(k - 1))
-
-        pass_on(nz // 2 - 1, False)
-        read_pair(nz // 2 - 1)
-        project(head_at(2 - nz // 2), head_at(nz // 2 - 2))
-        for i in order:
-            ag_arrived(nz // 2 - 1, 1 - first_way(i), i)
+            pass_on(k, True, later_work)
+            for i in range(pieces):
+                for d in (UP, DOWN):
+                    ag_copy(k - 3, d, i).wait_send()
+
+        pass_on(end - 1, False, later_work)
+        for slot in range(pieces):
+            read_slice(end - 1, slot)
+            project_slice(end - 2, slot)
+        own_copy().wait_send()
+        for k in (end - 4, end - 3):
+            for i in range(pieces):
+                for d in (UP, DOWN):
+                    ag_copy(k, d, i).wait_send()
+        for slot, i in enumerate(order):
+            ag_arrived(end - 1, 1 - first_way(i), i)
             if i == pieces - 1:
-                hand_copy(head_at(nz // 2)).start()
-        project(head_at(1 - nz // 2), head_at(nz // 2 - 1))
-        read_head(head_at(nz // 2), 0)
-        project(z, head_at(nz // 2), last=True)
-
-        own_copy().wait_send()
+                hand_copy(head_at(end)).start()
+            if slot < seqs:
+                for part_at in (2 * slot, 2 * slot + 1):
+                    project_slice(end - 1, part_at)
+            else:
+                read_part(head_at(end), 0, slot - seqs)
+        project(z, head_at(end), last=True)
+
         for i in range(pieces):
             rs_copy(0, first_way(i), i).wait_send()
-            ag_copy(nz // 2 - 1, 1 - first_way(i), i).wait_send()
-
-        @pl.loop(0, nz // 2 - 1)
-        def _(k):
-            for i in range(pieces):
-                for d in (UP, DOWN):
-                    rs_copy(k + 1, d, i).wait_send()
-                    ag_copy(k, d, i).wait_send()
+            for d in (UP, DOWN):
+                ag_copy(end - 2, d, i).wait_send()
+            ag_copy(end - 1, 1 - first_way(i), i).wait_send()
 
         @pl.loop(0, nz)
         def _(j):
@@ -347,8 +406,7 @@
 
     @pl.when(core == 0)
     def _weights():
-        for load in loads:
-            load.start()
+        start_loads()
         east, west = y * nx + lax.rem(x + 1, nx), y * nx + lax.rem(x + nx - 1, nx)
         north, south = lax.rem(y + 1, ny) * nx + x, lax.rem(y + ny - 1, ny) * nx + x
         ways = ((east, west), (north, south))
@@ -397,26 +455,28 @@
         def push(dx, dy, which):
             push_copy(at(dx, dy), which).start()
 
-        loads[0].wait()
-        loads[1].wait()
-        relayout_all()
+        relayout_first()
+        partial(head_at(nz // 2), seqs)
         pl.semaphore_wait(barrier, 5)
-        loads[4].wait()
-        send(0, 0)
-        send(1, 1)
+        part_copy(head_at(nz // 2)).start()
+        relayout_rest()
 
         def part_out(offset):
             partial(head_at(offset), seqs)
             part_copy(head_at(offset)).start()
 
-        part_out(nz // 2)
-
-        @pl.loop(1, nz // 2)
+        part_out(nz // 2 + 1)
+        part_out(nz // 2 - 1)
+        own_load.wait()
+        send(0, 0)
+        send(1, 1)
+
+        @pl.loop(2, nz // 2)
         def _(k):
             part_out(nz // 2 + k)
             part_out(nz // 2 - k)
 
-            @pl.when(k == 2)
+            @pl.when(k == 3)
             def _():
                 own_copy().wait_recv()
                 send(1, 0)
@@ -424,8 +484,8 @@
 
         part_out(0)
         push(0, 0, 0)
-        loads[2].wait()
-        loads[3].wait()
+        for load in late_loads:
+            load.wait()
 
         @pl.loop(0, late_units // 2)
         def _(i):
@@ -481,26 +541,6 @@
             got(0, item, 1)
             push(2, off, 1)
 
-        hand_copy(z).wait_recv()
-        read_head(z, seqs)
-
-        def read_pair(k):
-            for head in (head_at(-k), head_at(k)):
-                hand_copy(head).wait_recv()
-                read_head(head, seqs)
-
-        read_pair(1)
-        project(head_at(-1), head_at(1), first=True)
-
-        @pl.loop(2, nz // 2)
-        def _(k):
-            read_pair(k)
-            project(head_at(-k), head_at(k))
-
-        hand_copy(head_at(nz // 2)).wait_recv()
-        read_head(head_at(nz // 2), seqs)
-        project(z, head_at(nz // 2), last=True)
-
         for axis in (0, 1):
             for item in range(5):
                 for way in (0, 1):
@@ -511,11 +551,30 @@
         def _(j):
             part_copy(j).wait_send()
 
+        hand_copy(z).wait_recv()
+        read_head(z, seqs)
+
+        def read_pair(k):
+            for head in (head_at(-k), head_at(k)):
+                hand_copy(head).wait_recv()
+                read_head(head, seqs)
+
+        read_pair(1)
+        project(head_at(-1), head_at(1), first=True)
         for offset in range(nx * ny):
             piece = lax.rem(chip + offset, nx * ny)
             push_copy(piece, 0).wait_send()
             if offset > 0:
                 push_copy(piece, 1).wait_send()
+
+        @pl.loop(2, nz // 2)
+        def _(k):
+            read_pair(k)
+            project(head_at(-k), head_at(k))
+
+        hand_copy(head_at(nz // 2)).wait_recv()
+        read_head(head_at(nz // 2), seqs)
+        project(z, head_at(nz // 2), last=True)
 
 
 def local(ny, nx, nz, query_rows, key_rows, value_rows, gate_rows, out_weight):
@@ -531,7 +590,7 @@
         functools.partial(layer_kernel, ny, nx, nz, float(tokens * nz)),
         name="layer",
         out_shape=jax.ShapeDtypeStruct((seqs, tokens, width), BF16),
-        in_specs=[pl.BlockSpec(memory_space=pl.ANY)] * 5,
+        in_specs=[pl.BlockSpec(memory_space=pltpu.HBM)] * 5,
         out_specs=pl.BlockSpec(memory_space=pltpu.VMEM),
         scratch_shapes=[
             raw, raw, raw, raw,
@@ -543,7 +602,7 @@
             pltpu.VMEM((chips, 2 * rows, width), BF16),
             pltpu.VMEM((heads, seqs * tokens, size), BF16),
             pltpu.VMEM((seqs * tokens, width), F32),
-            dma((5,)),
+            dma((4, seqs)),
             dma((heads,)), dma((heads,)),
             dma((nz // 2, 2, 2 * seqs)), dma((nz // 2, 2, 2 * seqs)),
             dma((nz // 2, 2, 2 * seqs)), dma((nz // 2, 2, 2 * seqs)),
@@ -553,9 +612,9 @@
             dma, dma,
         ],
         compiler_params=pltpu.CompilerParams(
-            collective_id=0, has_side_effects=True, vmem_limit_bytes=60 * 2**20
+            collective_id=0, has_side_effects=True, vmem_limit_bytes=52 * 2**20
         ),
-    )(query_rows, key_rows, value_rows, gate_rows, out_weight)
+    )(query_rows, key_rows, value_rows, gate_rows, pltpu.with_memory_space_constraint(out_weight, pltpu.HBM))
 
 
 def solution(mesh):

time: 68.7 us -> 64.6 us (0.940)
  Pallas kernels: 65.8 us -> 63.3 us
  local copies, waits for them, and re-layouts: 2.73 us -> 1.15 us
    pallas_call x1, Pallas kernels: 65.8 us -> 63.3 us  [local(): pl.pallas_call(functools.partial(layer_kernel, ny, nx, nz, float(tokens *...]
    unnamed x1, local copies, waits for them, and re-layouts: 2.73 us -> 1.15 us
where the time goes in v2:
time: 64.6 us; the launch traced here: 64.5 us
  Pallas kernels  63.3 us (98%)
  local copies, waits for them, and re-layouts  1.15 us (2%)
    pallas_call x1, Pallas kernels, local(): pl.pallas_call(functools.partial(layer_kernel, ny, nx, nz, float(tokens *...  63.3 us

profile of v2, /device:TPU:1, one launch (start us, length us, event | category | flops | bytes accessed | tf_op | source)
XLA Modules:
  0.0 64.5 jit_solution(8306717476402956003)
XLA Ops:
  0.0 63.3 %layer.1 = bf16[2,192,2048]{2,1,0:T(8,128)(2,1)S(1)} custom-call(bf16[2,192,16,128]{3,2,1,0:T(8,128)(2,1)} %q_hbm.1, bf16[2,192,16,128]{3,2,1,0:T(8,128)(2,1)} %k_hbm.1, bf16[2,192,16,128]{3,2,1,0:T(8,128)(2,1)} %v_hbm.1, bf16[2,192,16,128]{3,2,1,0:T(8,128)(2,1)} %g_hbm.1, bf16[64,2048]{1,0:T(8,128)(2,1)} %w_hbm.1), custom_call_target="tpu_custom_call" | custom-call | tf_op jit(solution)/shard_map/layer/pallas_call | solution.py:589
  63.3 1.1 %copy.7 = bf16[2,192,2048]{2,1,0:T(8,128)(2,1)} copy(bf16[2,192,2048]{2,1,0:T(8,128)(2,1)S(1)} %layer.1) | data formatting | bytes 3145728

commit v3 on v2

--- a/solution.py
+++ b/solution.py
@@ -11,6 +11,11 @@
 F32, BF16 = jnp.float32, jnp.bfloat16
 BLOCK = 32
 UP, DOWN = 0, 1
+SIDE_FAR, SIDE_NEAR = 6, 7
+HOPS = (1, 1, 1, 1, 2, 2, 1, 1)
+ROLES = (8, 7, 6, 5, 4, 2, 3, 1)
+AG_HOPS = (2, 2, 1, 1, 1, 1, 1, 1)
+HELD = (0, 2, 4, 5, 6, 7, 2, 0)
 
 
 def feature(raw):
@@ -34,7 +39,6 @@
     core = lax.rem(f, 2)
     chip = f // 2
     x, y = lax.rem(chip, nx), chip // nx
-    above, below = lax.rem(z + 1, nz), lax.rem(z + nz - 1, nz)
     partner = {"fsdp": chip * 2 + 1 - core}
     barrier = pltpu.get_barrier_semaphore()
 
@@ -80,19 +84,37 @@
                     rows = pl.ds(pl.multiple_of(i * BLOCK, BLOCK), BLOCK)
                     dst[span, s, rows, :] = by_head(fn(src[s, rows, span])).astype(BF16)
 
+    def partials(which):
+        first_row = seqs * (1 - core)
+        ones = jnp.ones((8, tokens), BF16)
+        place = lax.broadcasted_iota(jnp.int32, (8, size), 0)
+        for head in range(which * group, (which + 1) * group):
+            mass = jnp.zeros((8, size), F32)
+            for s in range(seqs):
+                keys = k_feat[head, s]
+                part[head, s * size:(s + 1) * size, :] = lax.dot_general(
+                    keys, v_head[head, s], (((0,), (0,)), ((), ())), preferred_element_type=F32
+                )
+                row = jnp.dot(ones, keys, preferred_element_type=F32)
+                mass = jnp.where(place == first_row + s, row, mass)
+            part[head, seqs * size:, :] = mass
+
     starts_late = z >= nz // 2
 
-    def relayout_first():
+    def prepare_first():
         relayout(0, True)
+        partials(0)
 
         @pl.when(jnp.logical_not(starts_late))
         def _():
             relayout(1, False)
-
-    def relayout_rest():
+            partials(1)
+
+    def prepare_rest():
         @pl.when(starts_late)
         def _():
             relayout(1, False)
+            partials(1)
 
     def relayout_late(unit):
         per_seq = tokens // BLOCK
@@ -103,19 +125,6 @@
         gates[:, s, rows, :] = by_head(count**0.5 / (1.0 + jnp.exp(-gate)))
 
     late_units = seqs * tokens // BLOCK
-
-    def partial(head, first_row):
-        ones = jnp.ones((8, tokens), BF16)
-        place = lax.broadcasted_iota(jnp.int32, (8, size), 0)
-        mass = jnp.zeros((8, size), F32)
-        for s in range(seqs):
-            keys = k_feat[head, s]
-            part[head, s * size:(s + 1) * size, :] = lax.dot_general(
-                keys, v_head[head, s], (((0,), (0,)), ((), ())), preferred_element_type=F32
-            )
-            row = jnp.dot(ones, keys, preferred_element_type=F32)
-            mass = jnp.where(place == first_row + s, row, mass)
-        part[head, seqs * size:, :] = mass
 
     def read_part(head, first_row, s):
         tail = states[head, state_rows:, :].astype(F32)
@@ -135,7 +144,7 @@
 
     def project_part(a, b, i, first=False, last=False):
         rows = jnp.concatenate([mixed[a], mixed[b]], axis=1)
-        cols = pl.ds(pl.multiple_of(i * step, step), step)
+        cols = pl.ds(i * step, step)
         piece = jnp.dot(
             rows, jnp.concatenate([weight[a, :, cols], weight[b, :, cols]], axis=0),
             preferred_element_type=F32,
@@ -149,8 +158,7 @@
             total[:, cols] = piece
 
     def project(a, b, first=False, last=False):
-        @pl.loop(0, width // step)
-        def _(i):
+        for i in range(width // step):
             project_part(a, b, i, first, last)
 
     def part_copy(head):
@@ -183,42 +191,45 @@
     @pl.when(core == 1)
     def _ring():
         start_loads()
-        for device in ({"seq": above}, {"seq": below}, partner):
+        near = [{"seq": lax.rem(z + hop, nz)} for hop in (1, 2, nz - 2, nz - 1)]
+        for device in near + [partner]:
             pl.semaphore_signal(barrier, inc=1, device_id=device, device_id_type=MESH)
-        relayout_first()
-        partial(head_at(nz // 2), 0)
-        pl.semaphore_wait(barrier, 3)
+        prepare_first()
+        pl.semaphore_wait(barrier, 5)
         own_copy().start()
 
         pieces = 2 * seqs
         spans = [(i * size, size if i < pieces - 1 else size + 16) for i in range(pieces)]
         early = jnp.where(lax.rem(z, 4) < 2, DOWN, UP)
-
-        def target(d):
-            return {"seq": jnp.where(d == UP, above, below)}
-
-        def rs_copy(k, d, i):
+        both = (early, 1 - early)
+
+        def target(d, hop):
+            return {"seq": lax.rem(z + jnp.where(d == UP, hop, nz - hop), nz)}
+
+        def source(m):
+            return m if m < SIDE_FAR else 2 * m - 5
+
+        def rs_copy(m, d, i):
             rows = pl.ds(*spans[i])
             return pltpu.make_async_remote_copy(
-                sums.at[d, k, rows], sums.at[d, k + 1, rows], rs_send.at[k, d, i], rs_recv.at[k, d, i],
-                device_id=target(d), device_id_type=MESH,
+                sums.at[d, source(m), rows], sums.at[d, source(m) + 1, rows],
+                rs_send.at[m, d, i], rs_recv.at[m, d, i],
+                device_id=target(d, HOPS[m]), device_id_type=MESH,
             )
 
-        def ag_copy(k, d, i):
+        def ag_message(m, d, i, distance):
             rows = pl.ds(*spans[i])
-            head = head_at(jnp.where(d == UP, -k, k))
+            head = head_at(jnp.where(d == UP, -distance, distance))
             return pltpu.make_async_remote_copy(
-                states.at[head, rows], states.at[head, rows], ag_send.at[k, d, i], ag_recv.at[k, d, i],
-                device_id=target(d), device_id_type=MESH,
+                states.at[head, rows], states.at[head, rows], ag_send.at[m, d, i], ag_recv.at[m, d, i],
+                device_id=target(d, AG_HOPS[m]), device_id_type=MESH,
             )
 
-        def ag_arrived(k, d, i):
-            rows = pl.ds(*spans[i])
-            head = head_at(jnp.where(d == UP, -k - 1, k + 1))
-            pltpu.make_async_remote_copy(
-                states.at[head, rows], states.at[head, rows], ag_send.at[k, d, i], ag_recv.at[k, d, i],
-                device_id=target(d), device_id_type=MESH,
-            ).wait_recv()
+        def ag_copy(m, d, i):
+            return ag_message(m, d, i, HELD[m])
+
+        def ag_arrived(m, d, i):
+            ag_message(m, d, i, HELD[m] + AG_HOPS[m]).wait_recv()
 
         def own_sum(head, i):
             if i < seqs:
@@ -232,102 +243,125 @@
             high = mass.astype(BF16)
             return jnp.concatenate([high.astype(F32), mass - high.astype(F32)], axis=0).astype(BF16)
 
-        def add_and_send(k, d, i, received):
-            head = head_at(jnp.where(d == UP, nz // 2 - k, nz // 2 + k))
+        def add_and_send(m, d, i, received=()):
+            head = head_at(jnp.where(d == UP, ROLES[m], -ROLES[m]))
             start = i * size
+            slot = source(m)
             value = own_sum(head, i)
-            if received:
-                rs_copy(k - 1, d, i).wait_recv()
-                value = value + sums[d, k, start:start + size, :].astype(F32)
-            sums[d, k, start:start + size, :] = value.astype(BF16)
+            for r in received:
+                rs_copy(r, d, i).wait_recv()
+                value = value + sums[d, source(r) + 1, start:start + size, :].astype(F32)
+            sums[d, slot, start:start + size, :] = value.astype(BF16)
             if i == pieces - 1:
                 mass = own_mass(head)
-                if received:
-                    old = sums[d, k, state_rows:, :].astype(F32)
+                for r in received:
+                    old = sums[d, source(r) + 1, state_rows:, :].astype(F32)
                     mass = mass + old[:8] + old[8:]
-                sums[d, k, state_rows:, :] = split(mass)
-            rs_copy(k, d, i).start()
+                sums[d, slot, state_rows:, :] = split(mass)
+            rs_copy(m, d, i).start()
 
         def first_way(i):
             return DOWN if i < seqs else UP
+
+        def other_here(m):
+            part_copy(head_at(ROLES[m])).wait_recv()
+            part_copy(head_at(-ROLES[m])).wait_recv()
+
+        def side(m, some):
+            for i in some:
+                if i == seqs:
+                    other_here(m)
+                for d in both:
+                    add_and_send(m, d, i)
+
+        own_half, other_half = range(seqs), range(seqs, pieces)
 
         for i in range(pieces):
             if i == seqs:
                 part_copy(head_at(nz // 2)).wait_recv()
-            add_and_send(0, first_way(i), i, False)
-        relayout_rest()
-        partial(head_at(nz // 2 + 1), 0)
-        partial(head_at(nz // 2 - 1), 0)
+            add_and_send(0, first_way(i), i)
+        prepare_rest()
         for i in range(pieces):
             if i == seqs:
-                part_copy(head_at(nz // 2 + 1)).wait_recv()
-                part_copy(head_at(nz // 2 - 1)).wait_recv()
-            add_and_send(1, 1 - first_way(i), i, False)
-            add_and_send(1, first_way(i), i, True)
-        partial(head_at(nz // 2 + 2), 0)
-        partial(head_at(nz // 2 - 2), 0)
+                other_here(1)
+            add_and_send(1, 1 - first_way(i), i)
+            add_and_send(1, first_way(i), i, (0,))
+        side(SIDE_FAR, own_half)
         for load in late_loads:
             load.wait()
-
-        per_step = -(-late_units // (nz // 2 - 2))
-
-        @pl.loop(2, nz // 2)
-        def _(k):
+        sides = {2: (SIDE_FAR, other_half), 3: (SIDE_NEAR, own_half), 4: (SIDE_NEAR, other_half)}
+        for m in range(2, 6):
             for i in range(pieces):
                 if i == seqs:
-                    part_copy(head_at(nz // 2 + k)).wait_recv()
-                    part_copy(head_at(nz // 2 - k)).wait_recv()
-                add_and_send(k, early, i, True)
-                add_and_send(k, 1 - early, i, True)
-
-            @pl.when(k < nz // 2 - 1)
-            def _():
-                partial(head_at(nz // 2 + k + 1), 0)
-                partial(head_at(nz // 2 - k - 1), 0)
-
-            @pl.when(k == nz // 2 - 1)
-            def _():
-                partial(head_at(0), 0)
-
-            for j in range(per_step):
-                relayout_late((k - 2) * per_step + j)
-            rows = seqs * tokens // (nz // 2 - 2)
-            total[pl.ds(pl.multiple_of((k - 2) * rows, 8), rows), :] = jnp.zeros((rows, width), F32)
-
-        order = list(range(seqs, pieces)) + list(range(seqs))
+                    other_here(m)
+                for d in both:
+                    add_and_send(m, d, i, (m - 1, SIDE_FAR) if m == 5 else (m - 1,))
+            if m in sides:
+                side(*sides[m])
+
+            @pl.loop((m - 2) * late_units // 4, (m - 1) * late_units // 4)
+            def _(unit):
+                relayout_late(unit)
+
+        order = list(other_half) + list(own_half)
         part_copy(z).wait_recv()
         for i in order:
             start = i * size
             value = own_sum(z, i)
-            for d in (DOWN, UP):
-                rs_copy(nz // 2 - 1, d, i).wait_recv()
-                value = value + sums[d, nz // 2, start:start + size, :].astype(F32)
+            for m, d in ((SIDE_NEAR, DOWN), (SIDE_NEAR, UP), (5, DOWN), (5, UP)):
+                rs_copy(m, d, i).wait_recv()
+                value = value + sums[d, source(m) + 1, start:start + size, :].astype(F32)
             states[z, start:start + size, :] = (value * (1.0 / count)).astype(BF16)
             if i == pieces - 1:
                 mass = own_mass(z)
-                for d in (DOWN, UP):
-                    old = sums[d, nz // 2, state_rows:, :].astype(F32)
-                    mass = mass + old[:8] + old[8:]
+                for m in (SIDE_NEAR, 5):
+                    for d in (DOWN, UP):
+                        old = sums[d, source(m) + 1, state_rows:, :].astype(F32)
+                        mass = mass + old[:8] + old[8:]
                 states[z, state_rows:, :] = split(mass * (1.0 / count))
             ag_copy(0, UP, i).start()
             ag_copy(0, DOWN, i).start()
             if i == pieces - 1:
                 hand_copy(z).start()
 
-        def pass_on(k, both, work):
+        def hand_pair(distance):
+            hand_copy(head_at(-distance)).start()
+            hand_copy(head_at(distance)).start()
+
+        def pass_on(m, work, extra=None):
             for slot, i in enumerate(order):
-                if both:
-                    for d in (early, 1 - early):
-                        ag_arrived(k - 1, d, i)
-                        ag_copy(k, d, i).start()
+                if m < 5:
+                    for d in both:
+                        ag_arrived(m - 1, d, i)
+                        ag_copy(m, d, i).start()
                 else:
                     for d in (UP, DOWN):
-                        ag_arrived(k - 1, d, i)
-                    ag_copy(k, 1 - first_way(i), i).start()
+                        ag_arrived(m - 1, d, i)
+                    ag_copy(m, 1 - first_way(i), i).start()
                 if i == pieces - 1:
-                    hand_copy(head_at(-k)).start()
-                    hand_copy(head_at(k)).start()
-                work(k, slot)
+                    hand_pair(HELD[m])
+                for d in (UP, DOWN):
+                    rs_copy(m, d, i).wait_send()
+                if slot < pieces - 1:
+                    work(slot)
+            if extra is not None:
+                for i in extra[1]:
+                    for d in both:
+                        ag_copy(extra[0], d, i).start()
+            work(pieces - 1)
+
+        def side_came(m):
+            for i in order:
+                for d in both:
+                    ag_arrived(m, d, i)
+                if i == pieces - 1:
+                    hand_pair(HELD[m] + AG_HOPS[m])
+
+        def gone(*messages):
+            for m in messages:
+                for i in range(pieces):
+                    for d in (UP, DOWN):
+                        ag_copy(m, d, i).wait_send()
 
         def weights_here():
             own_load.wait()
@@ -337,68 +371,69 @@
                 if offset > 0:
                     push_copy(piece, 1).wait_recv()
 
-        def read_slice(k, slot):
-            read_part(head_at(-k) if slot < seqs else head_at(k), 0, slot % seqs)
-
-        def project_slice(k, slot):
-            project_part(head_at(-k), head_at(k), slot)
-
-        def drain(k, slot):
-            i = slot
-            for d in (UP, DOWN):
-                rs_copy(k, d, i).wait_send()
-
-        def first_work(k, slot):
-            drain(k, slot)
+        def read_slice(distance, slot):
+            read_part(head_at(-distance) if slot < seqs else head_at(distance), 0, slot % seqs)
+
+        def project_slice(distance, slot, first=False):
+            project_part(head_at(-distance), head_at(distance), slot, first)
+
+        def work_1(slot):
             if slot < seqs:
                 read_part(z, 0, slot)
 
-        def second_work(k, slot):
-            drain(k, slot)
-            read_slice(k - 1, slot)
-
-        def later_work(k, slot):
-            drain(k, slot)
-            read_slice(k - 1, slot)
-            project_slice(k - 2, slot)
-
+        def work_2(slot):
+            read_slice(2, slot)
+
+        def work_3(slot):
+            read_slice(4, slot)
+
+        def work_4(slot):
+            read_slice(5, slot)
+            project_slice(2, slot, True)
+            project_slice(4, slot)
+
+        def work_5(slot):
+            read_slice(6, slot)
+            read_slice(1, slot)
+            project_slice(5, slot)
+
+        pass_on(1, work_1, (SIDE_NEAR, other_half))
+        pass_on(2, work_2, (SIDE_NEAR, own_half))
+        pass_on(3, work_3, (SIDE_FAR, other_half))
+        weights_here()
+        pass_on(4, work_4, (SIDE_FAR, own_half))
+        side_came(SIDE_NEAR)
+        pass_on(5, work_5)
+        own_copy().wait_send()
+        for slot in range(pieces):
+            read_slice(7, slot)
+            project_slice(1, slot)
+        side_came(SIDE_FAR)
+        for slot in range(pieces):
+            read_slice(3, slot)
+            project_slice(6, slot)
+        for i in range(pieces):
+            rs_copy(0, first_way(i), i).wait_send()
+            for d in (UP, DOWN):
+                rs_copy(SIDE_FAR, d, i).wait_send()
+                rs_copy(SIDE_NEAR, d, i).wait_send()
+        gone(0, 1, 2, SIDE_NEAR)
         end = nz // 2
-        pass_on(1, True, first_work)
-        pass_on(2, True, second_work)
-        weights_here()
-
-        @pl.loop(3, end - 1)
-        def _(k):
-            pass_on(k, True, later_work)
-            for i in range(pieces):
-                for d in (UP, DOWN):
-                    ag_copy(k - 3, d, i).wait_send()
-
-        pass_on(end - 1, False, later_work)
-        for slot in range(pieces):
-            read_slice(end - 1, slot)
-            project_slice(end - 2, slot)
-        own_copy().wait_send()
-        for k in (end - 4, end - 3):
-            for i in range(pieces):
-                for d in (UP, DOWN):
-                    ag_copy(k, d, i).wait_send()
         for slot, i in enumerate(order):
-            ag_arrived(end - 1, 1 - first_way(i), i)
+            ag_arrived(5, 1 - first_way(i), i)
             if i == pieces - 1:
                 hand_copy(head_at(end)).start()
             if slot < seqs:
                 for part_at in (2 * slot, 2 * slot + 1):
-                    project_slice(end - 1, part_at)
+                    project_slice(7, part_at)
+                    project_slice(3, part_at)
             else:
                 read_part(head_at(end), 0, slot - seqs)
         project(z, head_at(end), last=True)
 
+        gone(3, 4, SIDE_FAR)
         for i in range(pieces):
-            rs_copy(0, first_way(i), i).wait_send()
-            for d in (UP, DOWN):
-                ag_copy(end - 2, d, i).wait_send()
-            ag_copy(end - 1, 1 - first_way(i), i).wait_send()
+            ag_copy(5, 1 - first_way(i), i).wait_send()
 
         @pl.loop(0, nz)
         def _(j):
@@ -455,34 +490,25 @@
         def push(dx, dy, which):
             push_copy(at(dx, dy), which).start()
 
-        relayout_first()
-        partial(head_at(nz // 2), seqs)
+        prepare_first()
         pl.semaphore_wait(barrier, 5)
         part_copy(head_at(nz // 2)).start()
-        relayout_rest()
-
-        def part_out(offset):
-            partial(head_at(offset), seqs)
-            part_copy(head_at(offset)).start()
-
-        part_out(nz // 2 + 1)
-        part_out(nz // 2 - 1)
+        prepare_rest()
+
+        part_order = (7, 3, 6, 5, 1, 4, 2)
+        for distance in part_order[:2]:
+            part_copy(head_at(-distance)).start()
+            part_copy(head_at(distance)).start()
         own_load.wait()
         send(0, 0)
         send(1, 1)
-
-        @pl.loop(2, nz // 2)
-        def _(k):
-            part_out(nz // 2 + k)
-            part_out(nz // 2 - k)
-
-            @pl.when(k == 3)
-            def _():
-                own_copy().wait_recv()
-                send(1, 0)
-                send(0, 1)
-
-        part_out(0)
+        for distance in part_order[2:]:
+            part_copy(head_at(-distance)).start()
+            part_copy(head_at(distance)).start()
+        part_copy(z).start()
+        own_copy().wait_recv()
+        send(1, 0)
+        send(0, 1)
         push(0, 0, 0)
         for load in late_loads:
             load.wait()
@@ -559,16 +585,15 @@
                 hand_copy(head).wait_recv()
                 read_head(head, seqs)
 
-        read_pair(1)
-        project(head_at(-1), head_at(1), first=True)
+        read_pair(2)
+        project(head_at(-2), head_at(2), first=True)
         for offset in range(nx * ny):
             piece = lax.rem(chip + offset, nx * ny)
             push_copy(piece, 0).wait_send()
             if offset > 0:
                 push_copy(piece, 1).wait_send()
 
-        @pl.loop(2, nz // 2)
-        def _(k):
+        for k in (4, 5, 1, 6, 7, 3):
             read_pair(k)
             project(head_at(-k), head_at(k))
 
@@ -597,15 +622,15 @@
             split, split, split,
             pltpu.VMEM((heads, seqs, tokens, size), F32),
             part, part,
-            pltpu.VMEM((2, nz // 2 + 1, chunk, size), BF16),
+            pltpu.VMEM((2, 11, chunk, size), BF16),
             pltpu.VMEM((heads, chunk, size), BF16),
             pltpu.VMEM((chips, 2 * rows, width), BF16),
             pltpu.VMEM((heads, seqs * tokens, size), BF16),
             pltpu.VMEM((seqs * tokens, width), F32),
             dma((4, seqs)),
             dma((heads,)), dma((heads,)),
-            dma((nz // 2, 2, 2 * seqs)), dma((nz // 2, 2, 2 * seqs)),
-            dma((nz // 2, 2, 2 * seqs)), dma((nz // 2, 2, 2 * seqs)),
+            dma((8, 2, 2 * seqs)), dma((8, 2, 2 * seqs)),
+            dma((8, 2, 2 * seqs)), dma((8, 2, 2 * seqs)),
             dma((heads,)), dma((heads,)),
             dma((2, 5, 2, 2)), dma((2, 5, 2, 2)),
             dma((chips, 2)), dma((chips, 2)),

time: 64.6 us -> 60.1 us (0.930)
  Pallas kernels: 63.3 us -> 58.8 us
    pallas_call x1, Pallas kernels: 63.3 us -> 58.8 us  [local(): pl.pallas_call(functools.partial(layer_kernel, ny, nx, nz, float(tokens *...]
where the time goes in v3:
time: 60.1 us; the launch traced here: 60 us
  Pallas kernels  58.8 us (98%)
  local copies, waits for them, and re-layouts  1.15 us (2%)
    pallas_call x1, Pallas kernels, local(): pl.pallas_call(functools.partial(layer_kernel, ny, nx, nz, float(tokens *...  58.8 us

profile of v3, /device:TPU:1, one launch (start us, length us, event | category | flops | bytes accessed | tf_op | source)
XLA Modules:
  0.0 60.0 jit_solution(5518041747798438147)
XLA Ops:
  0.0 58.8 %layer.1 = bf16[2,192,2048]{2,1,0:T(8,128)(2,1)S(1)} custom-call(bf16[2,192,16,128]{3,2,1,0:T(8,128)(2,1)} %q_hbm.1, bf16[2,192,16,128]{3,2,1,0:T(8,128)(2,1)} %k_hbm.1, bf16[2,192,16,128]{3,2,1,0:T(8,128)(2,1)} %v_hbm.1, bf16[2,192,16,128]{3,2,1,0:T(8,128)(2,1)} %g_hbm.1, bf16[64,2048]{1,0:T(8,128)(2,1)} %w_hbm.1), custom_call_target="tpu_custom_call" | custom-call | tf_op jit(solution)/shard_map/layer/pallas_call | solution.py:614
  58.8 1.1 %copy.7 = bf16[2,192,2048]{2,1,0:T(8,128)(2,1)} copy(bf16[2,192,2048]{2,1,0:T(8,128)(2,1)S(1)} %layer.1) | data formatting | bytes 3145728

commit v4 on v3

--- a/solution.py
+++ b/solution.py
@@ -328,7 +328,12 @@
             hand_copy(head_at(-distance)).start()
             hand_copy(head_at(distance)).start()
 
-        def pass_on(m, work, extra=None):
+        def side_copies(m, some):
+            for i in some:
+                for d in both:
+                    ag_copy(m, d, i).start()
+
+        def pass_on(m, work, extra=()):
             for slot, i in enumerate(order):
                 if m < 5:
                     for d in both:
@@ -344,10 +349,8 @@
                     rs_copy(m, d, i).wait_send()
                 if slot < pieces - 1:
                     work(slot)
-            if extra is not None:
-                for i in extra[1]:
-                    for d in both:
-                        ag_copy(extra[0], d, i).start()
+            for side_m, some in extra:
+                side_copies(side_m, some)
             work(pieces - 1)
 
         def side_came(m):
@@ -389,29 +392,31 @@
 
         def work_4(slot):
             read_slice(5, slot)
+            read_slice(1, slot)
             project_slice(2, slot, True)
             project_slice(4, slot)
 
         def work_5(slot):
             read_slice(6, slot)
-            read_slice(1, slot)
+            read_slice(3, slot)
             project_slice(5, slot)
-
-        pass_on(1, work_1, (SIDE_NEAR, other_half))
-        pass_on(2, work_2, (SIDE_NEAR, own_half))
-        pass_on(3, work_3, (SIDE_FAR, other_half))
+            project_slice(1, slot)
+
+        side_copies(SIDE_NEAR, other_half)
+        pass_on(1, work_1, ((SIDE_NEAR, own_half),))
+        pass_on(2, work_2, ((SIDE_FAR, other_half),))
+        pass_on(3, work_3, ((SIDE_FAR, own_half),))
         weights_here()
-        pass_on(4, work_4, (SIDE_FAR, own_half))
         side_came(SIDE_NEAR)
+        pass_on(4, work_4, ())
+        side_came(SIDE_FAR)
         pass_on(5, work_5)
         own_copy().wait_send()
         for slot in range(pieces):
             read_slice(7, slot)
-            project_slice(1, slot)
-        side_came(SIDE_FAR)
+            project_slice(6, slot)
         for slot in range(pieces):
-            read_slice(3, slot)
-            project_slice(6, slot)
+            project_slice(3, slot)
         for i in range(pieces):
             rs_copy(0, first_way(i), i).wait_send()
             for d in (UP, DOWN):
@@ -426,7 +431,6 @@
             if slot < seqs:
                 for part_at in (2 * slot, 2 * slot + 1):
                     project_slice(7, part_at)
-                    project_slice(3, part_at)
             else:
                 read_part(head_at(end), 0, slot - seqs)
         project(z, head_at(end), last=True)
@@ -513,7 +517,7 @@
         for load in late_loads:
             load.wait()
 
-        @pl.loop(0, late_units // 2)
+        @pl.loop(0, late_units)
         def _(i):
             relayout_late(i)
 
@@ -527,10 +531,6 @@
         send(0, 3)
         push(0, -1, 1)
         push(0, 1, 1)
-
-        @pl.loop(late_units // 2, late_units)
-        def _(i):
-            relayout_late(i)
 
         forward(0, 1)
         forward(1, 1)
@@ -593,7 +593,7 @@
             if offset > 0:
                 push_copy(piece, 1).wait_send()
 
-        for k in (4, 5, 1, 6, 7, 3):
+        for k in (4, 5, 1, 6, 3, 7):
             read_pair(k)
             project(head_at(-k), head_at(k))
 

time: 60.1 us -> 59.1 us (0.983)
  Pallas kernels: 58.8 us -> 57.9 us
    pallas_call x1, Pallas kernels: 58.8 us -> 57.9 us  [local(): pl.pallas_call(functools.partial(layer_kernel, ny, nx, nz, float(tokens *...]
where the time goes in v4:
time: 59.1 us; the launch traced here: 59 us
  Pallas kernels  57.9 us (98%)
  local copies, waits for them, and re-layouts  1.15 us (2%)
    pallas_call x1, Pallas kernels, local(): pl.pallas_call(functools.partial(layer_kernel, ny, nx, nz, float(tokens *...  57.9 us

profile of v4, /device:TPU:1, one launch (start us, length us, event | category | flops | bytes accessed | tf_op | source)
XLA Modules:
  0.0 59.0 jit_solution(2343752454763660754)
XLA Ops:
  0.0 57.9 %layer.1 = bf16[2,192,2048]{2,1,0:T(8,128)(2,1)S(1)} custom-call(bf16[2,192,16,128]{3,2,1,0:T(8,128)(2,1)} %q_hbm.1, bf16[2,192,16,128]{3,2,1,0:T(8,128)(2,1)} %k_hbm.1, bf16[2,192,16,128]{3,2,1,0:T(8,128)(2,1)} %v_hbm.1, bf16[2,192,16,128]{3,2,1,0:T(8,128)(2,1)} %g_hbm.1, bf16[64,2048]{1,0:T(8,128)(2,1)} %w_hbm.1), custom_call_target="tpu_custom_call" | custom-call | tf_op jit(solution)/shard_map/layer/pallas_call | solution.py:614
  57.9 1.1 %copy.7 = bf16[2,192,2048]{2,1,0:T(8,128)(2,1)} copy(bf16[2,192,2048]{2,1,0:T(8,128)(2,1)S(1)} %layer.1) | data formatting | bytes 3145728
